TPU v7x, 32 devices: a whole 2x2x4 slice. The times are simulated.
32 devices in a mesh: ba: 8 (over z, x), ka: 4 (over y, core).
Axes of the slice: x: 2, y: 2, z: 4, core: 2. Of those that a mesh axis runs over, the one named last changes fastest.
Arguments:
- emb_one: bfloat16 [8192, 128], P('ba'), may hold values from -8 to 8, as said below
- emb_two: bfloat16 [8192, 128], P('ba'), may hold values from -8 to 8, as said below
- prototypes: float32 [3000, 128], P('ka', 'ba'), may hold values from -6 to 6, as said below
Outputs:
- assignment_weights: float32 [8192, 3000], P('ba', 'ka')
- row_loss: float32 [8192], P('ba')
Inputs may be any that keep to these rules, and one draw needn't show every extreme that they name: `prototypes`: prototype entries are finite and lie within the stated range. `emb_one`: embedding entries are finite and lie within the stated range; rows are not zero. `emb_two`: embedding entries are finite and lie within the stated range; rows are not zero.
All inputs are finite; a program needn't handle non-finite values.
Results may differ from a plain program's by a relative error of at most 0.0003.
Values sent between devices are 32-bit elements.
A program may use at most 64 MiB of HBM per device.

v0:
```python
import jax
import jax.numpy as jnp
from jax import lax
from jax.sharding import PartitionSpec as P

K = 3000
REPEAT_COUNT = 3
TEMP_CODE = 0.05
TEMP_PRED = 0.1


def unit_rows(values):
    values = values.astype(jnp.float32)
    factor = lax.rsqrt(jnp.sum(values * values, axis=1, keepdims=True))
    return (values * factor).astype(jnp.bfloat16)


def vector_columns(current):
    kernel, col_scale, row_scale = current
    return (
        jnp.sum(kernel[0] * row_scale[0][:, None], axis=0),
        jnp.sum(kernel[1] * row_scale[1][:, None], axis=0),
    )


def vector_by_columns(current, totals):
    return (current[0], (1.0 / totals[0], 1.0 / totals[1]), current[2])


def vector_samples(current):
    kernel, col_scale, row_scale = current
    return (
        jnp.sum(kernel[0] * col_scale[0][None, :], axis=1),
        jnp.sum(kernel[1] * col_scale[1][None, :], axis=1),
    )


def vector_by_samples(current, totals):
    return (current[0], current[1], (1.0 / totals[0], 1.0 / totals[1]))


def vector_raw(current):
    kernel, col_scale, row_scale = current
    return (
        kernel[0] * col_scale[0][None, :] * row_scale[0][:, None],
        kernel[1] * col_scale[1][None, :] * row_scale[1][:, None],
    )


def body(emb_one, emb_two, prototypes):
    gathered = lax.all_gather(prototypes, "ba", axis=1, tiled=True)
    centers = unit_rows(gathered)
    first_view_logits = jnp.dot(unit_rows(emb_one), centers.T, preferred_element_type=jnp.float32)
    second_view_logits = jnp.dot(unit_rows(emb_two), centers.T, preferred_element_type=jnp.float32)
    kernel = (jnp.exp(first_view_logits / TEMP_CODE), jnp.exp(second_view_logits / TEMP_CODE))
    column_part, column_apply = (vector_columns, vector_by_columns)
    sample_part, sample_apply, raw_matrix = (vector_samples, vector_by_samples, vector_raw)
    col_ones = jnp.ones((first_view_logits.shape[1],), jnp.float32)
    row_ones = jnp.ones((first_view_logits.shape[0],), jnp.float32)
    current = (kernel, (col_ones, col_ones), (row_ones, row_ones))
    for iteration in range(REPEAT_COUNT):
        partial_sums = column_part(current)
        totals = lax.psum((partial_sums[0], partial_sums[1]), "ba")
        current = column_apply(current, totals)
        if iteration + 1 < REPEAT_COUNT:
            partial_sums = sample_part(current)
            totals = lax.psum((partial_sums[0], partial_sums[1]), "ka")
            current = sample_apply(current, totals)
    raw_one, raw_two = raw_matrix(current)
    logit_one = first_view_logits / TEMP_PRED
    logit_two = second_view_logits / TEMP_PRED
    masses = lax.psum((jnp.sum(raw_one, axis=1), jnp.sum(raw_two, axis=1)), "ka")
    first_view_assignment = raw_one / masses[0][:, None]
    second_view_assignment = raw_two / masses[1][:, None]
    peaks = lax.pmax((jnp.max(logit_one, axis=1), jnp.max(logit_two, axis=1)), "ka")
    terms = lax.psum(
        (
            jnp.sum(jnp.exp(logit_one - peaks[0][:, None]), axis=1),
            jnp.sum(jnp.exp(logit_two - peaks[1][:, None]), axis=1),
            jnp.sum(first_view_assignment * logit_two, axis=1),
            jnp.sum(second_view_assignment * logit_one, axis=1),
        ),
        "ka",
    )
    lse_one = peaks[0] + jnp.log(terms[0])
    lse_two = peaks[1] + jnp.log(terms[1])
    row_loss = lse_two - terms[2] + lse_one - terms[3]
    return (K * first_view_assignment, row_loss)


def solution(mesh):
    placed = (P("ba", None), P("ba", None), P("ka", "ba"))
    return jax.shard_map(
        body, mesh=mesh, in_specs=placed, out_specs=(P("ba", "ka"), P("ba")), check_vma=False
    )
```

profile of v0, /device:TPU:0, one launch (start us, length us, event | category | flops | bytes accessed | tf_op | source)
XLA Modules:
  0.0 154.9 jit_solution(16839468313270747781)
XLA Ops:
  0.6 0.0 copy-start.1
  0.6 1.2 fusion.5
  1.9 1.2 fusion.7
  3.0 33.0 %all_gather.3 = f32[750,128]{0,1:T(8,128)S(1)} all-gather(f32[750,16]{0,1:T(8,128)} %param.5), channel_id=1, replica_groups=mesh['ba'=8,'ka'=4] {'ba'}, dimensions={1}, use_global_device_ids=true | all-gather | bytes 432000 | tf_op jit(solution)/shard_map/all_gather | solution.py:51
  36.1 1.7 %fusion.3 = (f32[750]{0:T(1024)S(1)}, f32[1024,750]{0,1:T(8,128)S(1)}) fusion(f32[750,128]{0,1:T(8,128)S(1)} %all_gather.3, f32[750]{0:T(1024)S(1)} %rsqrt.25, bf16[1024,128]{1,0:T(8,128)(2,1)} %param.3, f32[1024]{0:T(1024)S(1)} %rsqrt.24), kind=kOutput, calls=%fused_computation.22 | convolution fusion | flops 198728464 | bytes 3728240 | tf_op jit(solution)/shard_map/dot_general | solution.py:53
  37.8 0.0 copy-done.1
  37.8 2.6 %multiply_reduce_fusion.11 = (f32[1024]{0:T(1024)S(1)}, f32[750]{0:T(1024)S(1)}, f32[1024,750]{0,1:T(8,128)}) fusion(f32[750,128]{0,1:T(8,128)S(1)} %all_gather.3, f32[750]{0:T(1024)S(1)} %rsqrt.25, bf16[1024,128]{1,0:T(8,128)(2,1)S(1)} %copy-done.1, f32[1024]{0:T(1024)S(1)} %rsqrt.26), kind=kOutput, calls=%fused_computation.20 | convolution fusion | flops 200263440 | bytes 3732336 | tf_op jit(solution)/shard_map/dot_general | solution.py:54
  40.4 21.7 %all-reduce.2 = (f32[750]{0:T(1024)S(1)}, f32[750]{0:T(1024)S(1)}) all-reduce(f32[750]{0:T(1024)S(1)} %get-tuple-element.30, f32[750]{0:T(1024)S(1)} %get-tuple-element.7), channel_id=1, replica_groups=mesh['ba'=8,'ka'=4] {'ba'}, use_global_device_ids=true, to_apply=%region_3.0 | all-reduce | flops 1500 | bytes 12000 | tf_op jit(solution)/shard_map/psum | solution.py:63
  62.1 0.7 multiply_reduce_fusion.10
  62.8 5.8 %all-reduce.7 = (f32[1024]{0:T(1024)S(1)}, f32[1024]{0:T(1024)S(1)}) all-reduce(f32[1024]{0:T(1024)S(1)} %get-tuple-element.6, f32[1024]{0:T(1024)S(1)} %get-tuple-element.9), channel_id=1, replica_groups=mesh['ba'=8,'ka'=4] {'ka'}, use_global_device_ids=true, to_apply=%region_16.0 | all-reduce | flops 2048 | bytes 16384 | tf_op jit(solution)/shard_map/pmax | solution.py:75
  68.6 2.9 %exponential_reduce_fusion.1 = (f32[1024]{0:T(1024)S(1)}, f32[1024]{0:T(1024)S(1)}) fusion(f32[1024,750]{0,1:T(8,128)} %get-tuple-element.32, f32[1024]{0:T(1024)S(1)} %get-tuple-element.27, f32[750]{0:T(1024)S(1)} %broadcast_divide_fusion.6), kind=kLoop, calls=%fused_computation.9 | loop fusion | flops 4605952 | bytes 3087288 | tf_op jit(solution)/shard_map/reduce_sum | solution.py:79
  71.5 6.7 %all-reduce.6 = (f32[1024]{0:T(1024)S(1)}, f32[1024]{0:T(1024)S(1)}) all-reduce(f32[1024]{0:T(1024)S(1)} %get-tuple-element.10, f32[1024]{0:T(1024)S(1)} %get-tuple-element.5), channel_id=1, replica_groups=mesh['ba'=8,'ka'=4] {'ka'}, use_global_device_ids=true, to_apply=%region_5.0 | all-reduce | flops 2048 | bytes 16384 | tf_op jit(solution)/shard_map/psum | solution.py:67
  78.2 2.4 %multiply_reduce_fusion.3 = f32[750]{0:T(1024)S(1)} fusion(f32[1024]{0:T(1024)S(1)} %get-tuple-element.33, f32[1024,750]{0,1:T(8,128)} %get-tuple-element.32), kind=kLoop, calls=%fused_computation.4 | loop fusion | flops 2303250 | bytes 3079096 | tf_op jit(solution)/shard_map/reduce_sum | solution.py:22
  80.7 0.6 multiply_reduce_fusion.8
  81.3 17.4 %all-reduce.1 = (f32[750]{0:T(1024)S(1)}, f32[750]{0:T(1024)S(1)}) all-reduce(f32[750]{0:T(1024)S(1)} %multiply_reduce_fusion.8, f32[750]{0:T(1024)S(1)} %multiply_reduce_fusion.3), channel_id=1, replica_groups=mesh['ba'=8,'ka'=4] {'ba'}, use_global_device_ids=true, to_apply=%region_7.0 | all-reduce | flops 1500 | bytes 12000 | tf_op jit(solution)/shard_map/psum | solution.py:63
  98.6 0.0 copy-start
  98.7 0.5 multiply_reduce_fusion.7
  99.2 1.3 copy-done
  100.5 0.5 multiply_reduce_fusion.2
  101.1 5.8 %all-reduce.5 = (f32[1024]{0:T(1024)S(1)}, f32[1024]{0:T(1024)S(1)}) all-reduce(f32[1024]{0:T(1024)S(1)} %multiply_reduce_fusion.7, f32[1024]{0:T(1024)S(1)} %multiply_reduce_fusion.2), channel_id=1, replica_groups=mesh['ba'=8,'ka'=4] {'ka'}, use_global_device_ids=true, to_apply=%region_9.0 | all-reduce | flops 2048 | bytes 16384 | tf_op jit(solution)/shard_map/psum | solution.py:67
  106.9 2.4 %multiply_reduce_fusion.1 = f32[750]{0:T(1024)S(1)} fusion(f32[1024]{0:T(1024)S(1)} %broadcast_divide_fusion, f32[1024,750]{0,1:T(8,128)} %get-tuple-element.32), kind=kLoop, calls=%fused_computation.2 | loop fusion | flops 2303250 | bytes 3079096 | tf_op jit(solution)/shard_map/reduce_sum | solution.py:22
  109.3 0.6 multiply_reduce_fusion.6
  109.9 19.4 %all-reduce = (f32[750]{0:T(1024)S(1)}, f32[750]{0:T(1024)S(1)}) all-reduce(f32[750]{0:T(1024)S(1)} %multiply_reduce_fusion.6, f32[750]{0:T(1024)S(1)} %multiply_reduce_fusion.1), channel_id=1, replica_groups=mesh['ba'=8,'ka'=4] {'ba'}, use_global_device_ids=true, to_apply=%region_11.0 | all-reduce | flops 1500 | bytes 12000 | tf_op jit(solution)/shard_map/psum | solution.py:63
  129.3 2.5 %fusion.2 = f32[1024]{0:T(1024)S(1)} fusion(f32[750]{0:T(1024)S(1)} %broadcast_divide_fusion.4, f32[1024]{0:T(1024)S(1)} %broadcast_divide_fusion, f32[1024,750]{0,1:T(8,128)} %get-tuple-element.32), kind=kLoop, calls=%fused_computation.18 | loop fusion | flops 3070976 | bytes 3083192 | tf_op jit(solution)/shard_map/reduce_sum | solution.py:72
  131.8 0.6 fusion.1
  132.4 5.8 %all-reduce.4 = (f32[1024]{0:T(1024)S(1)}, f32[1024]{0:T(1024)S(1)}) all-reduce(f32[1024]{0:T(1024)S(1)} %fusion.1, f32[1024]{0:T(1024)S(1)} %fusion.2), channel_id=1, replica_groups=mesh['ba'=8,'ka'=4] {'ka'}, use_global_device_ids=true, to_apply=%region_13.0 | all-reduce | flops 2048 | bytes 16384 | tf_op jit(solution)/shard_map/psum | solution.py:72
  138.2 5.4 %multiply_reduce_fusion.5 = (f32[1024]{0:T(1024)S(1)}, f32[1024]{0:T(1024)S(1)}, f32[1024]{0:T(1024)S(1)}, f32[1024,750]{0,1:T(8,128)}) fusion(f32[1024,750]{0,1:T(8,128)} %get-tuple-element.32, f32[1024]{0:T(1024)S(1)} %get-tuple-element.21, f32[1024]{0:T(1024)S(1)} %broadcast_divide_fusion.2, f32[750]{0:T(1024)S(1)} %broadcast_divide_fusion.7, ...), kind=kLoop, calls=%fused_computation.8 | loop fusion | flops 13052928 | bytes 9254768 | tf_op jit(solution)/shard_map/reduce_sum | solution.py:80
  143.7 10.6 %all-reduce.3 = (f32[1024]{0:T(1024)S(1)}, f32[1024]{0:T(1024)S(1)}, f32[1024]{0:T(1024)S(1)}, f32[1024]{0:T(1024)S(1)}) all-reduce(f32[1024]{0:T(1024)S(1)} %get-tuple-element.3, f32[1024]{0:T(1024)S(1)} %get-tuple-element.8, f32[1024]{0:T(1024)S(1)} %get-tuple-element.2, ...), channel_id=1, replica_groups=mesh['ba'=8,'ka'=4] {'ka'}, use_global_device_ids=true, to_apply=%region_38.0 | all-reduce | flops 4096 | bytes 32768 | tf_op jit(solution)/shard_map/psum | solution.py:76
  154.3 0.6 add_subtract_fusion
  (13 shorter events, 0.1 us)
Async XLA Ops:
  0.6 37.2 %copy-start.1 = (bf16[1024,128]{1,0:T(8,128)(2,1)S(1)}, bf16[1024,128]{1,0:T(8,128)(2,1)}, u32[]{:S(2)}) copy-start(bf16[1024,128]{1,0:T(8,128)(2,1)} %param.4) | copy-start | bytes 786436
  98.6 1.9 %copy-start = (f32[1024,750]{0,1:T(8,128)S(1)}, f32[1024,750]{0,1:T(8,128)}, u32[]{:S(2)}) copy-start(f32[1024,750]{0,1:T(8,128)} %get-tuple-element.32) | copy-start | bytes 9216004
where the time goes:
time: 155 us
  blocking collectives  126 us (81%)
  other arithmetic  22.3 us (14%)
  matrix products  4.31 us (3%)
    psum x3, blocking collectives, body(): totals = lax.psum((partial_sums[0], partial_sums[1]), 'ba')  58.4 us
    all_gather x1, blocking collectives, body(): gathered = lax.all_gather(prototypes, 'ba', axis=1, tiled=True)  33 us
    psum x2, blocking collectives, body(): totals = lax.psum((partial_sums[0], partial_sums[1]), 'ka')  12.5 us
    psum x1, blocking collectives, body(): lax.psum((jnp.sum(jnp.exp(logit_one - peaks[0][:, None]), axis=1), jnp.su...  10.6 us
    pmax x1, blocking collectives, body(): lax.pmax((jnp.max(logit_one, axis=1), jnp.max(logit_two, axis=1)), 'ka')  5.77 us
    psum x1, blocking collectives, body(): lax.psum((jnp.sum(raw_one, axis=1), jnp.sum(raw_two, axis=1)), 'ka')  5.77 us
    reduce_sum x1, other arithmetic, body(): jnp.sum(first_view_assignment * logit_two, axis=1)  5.44 us
    reduce_sum x2, other arithmetic, vector_columns(): jnp.sum(kernel[1] * row_scale[1][:, None], axis=0)  4.9 us

commit v1 on v0

--- a/solution.py
+++ b/solution.py
@@ -7,6 +7,16 @@
 REPEAT_COUNT = 3
 TEMP_CODE = 0.05
 TEMP_PRED = 0.1
+
+
+def around_the_ring(x, mesh_axis, dim):
+    devices = lax.axis_size(mesh_axis)
+    current, blocks = (x, [x])
+    for _ in range(devices - 1):
+        current = lax.ppermute(current, mesh_axis, [(i, (i + 1) % devices) for i in range(devices)])
+        blocks.insert(0, current)
+    line = jnp.concatenate(blocks, axis=dim)
+    return jnp.roll(line, (lax.axis_index(mesh_axis) + 1) * x.shape[dim], axis=dim)
 
 
 def unit_rows(values):
@@ -48,7 +58,7 @@
 
 
 def body(emb_one, emb_two, prototypes):
-    gathered = lax.all_gather(prototypes, "ba", axis=1, tiled=True)
+    gathered = around_the_ring(prototypes, "ba", 1)
     centers = unit_rows(gathered)
     first_view_logits = jnp.dot(unit_rows(emb_one), centers.T, preferred_element_type=jnp.float32)
     second_view_logits = jnp.dot(unit_rows(emb_two), centers.T, preferred_element_type=jnp.float32)

time: 155 us -> 167 us (1.077)
  waiting for transfers between devices: 0 us -> 44 us
  blocking collectives: 126 us -> 89 us
  starting transfers between devices: 0 us -> 3.04 us
  local copies, waits for them, and re-layouts: 1.32 us -> 3.02 us
    ppermute x0 -> x7, waiting for transfers between devices: none -> 44 us  [around_the_ring(): lax.ppermute(current, mesh_axis, [(i, (i + 1) % devices) for i in range(d...]
    all_gather x1 -> x0, blocking collectives: 33 us -> none  [body(): gathered = lax.all_gather(prototypes, 'ba', axis=1, tiled=True)]
    psum x3, blocking collectives: 58.4 us -> 54.1 us  [body(): totals = lax.psum((partial_sums[0], partial_sums[1]), 'ba')]
    ppermute x0 -> x7, starting transfers between devices: none -> 3.04 us  [around_the_ring(): lax.ppermute(current, mesh_axis, [(i, (i + 1) % devices) for i in range(d...]
  transfers between devices with their start and end apart: 0 -> 7, of which waited for: 0 -> 7; matrix products, arithmetic and copies ran while one was open for 0% -> 1% of each run, Pallas kernels for 0% -> 0%
where the time goes in v1:
time: 167 us
  blocking collectives  89 us (53%)
  waiting for transfers between devices  44 us (26%)
  other arithmetic  22.3 us (13%)
  matrix products  4.31 us (3%)
  starting transfers between devices  3.04 us (2%)
  local copies, waits for them, and re-layouts  3.02 us (2%)
    psum x3, blocking collectives, body(): totals = lax.psum((partial_sums[0], partial_sums[1]), 'ba')  54.1 us
    ppermute x7, waiting for transfers between devices, around_the_ring(): lax.ppermute(current, mesh_axis, [(i, (i + 1) % devices) for i in range(d...  44 us
    psum x2, blocking collectives, body(): totals = lax.psum((partial_sums[0], partial_sums[1]), 'ka')  12.9 us
    psum x1, blocking collectives, body(): lax.psum((jnp.sum(jnp.exp(logit_one - peaks[0][:, None]), axis=1), jnp.su...  10.5 us
    pmax x1, blocking collectives, body(): lax.pmax((jnp.max(logit_one, axis=1), jnp.max(logit_two, axis=1)), 'ka')  5.77 us
    psum x1, blocking collectives, body(): lax.psum((jnp.sum(raw_one, axis=1), jnp.sum(raw_two, axis=1)), 'ka')  5.77 us
    reduce_sum x1, other arithmetic, body(): jnp.sum(first_view_assignment * logit_two, axis=1)  5.44 us
    reduce_sum x2, other arithmetic, vector_columns(): jnp.sum(kernel[1] * row_scale[1][:, None], axis=0)  4.9 us
  transfers between devices with their start and end apart: 7, of which 7 were waited for; matrix products, arithmetic and copies ran while one was open for 1% of the time, Pallas kernels for 0%

profile of v1, /device:TPU:0, one launch (start us, length us, event | category | flops | bytes accessed | tf_op | source)
XLA Modules:
  0.0 166.6 jit_solution(8660189559560051593)
XLA Ops:
  0.6 3.0 %collective-permute-start = (f32[750,16]{0,1:T(8,128)}, f32[750,16]{0,1:T(8,128)S(1)}, u32[]{:S(2)}, u32[]{:S(2)}) collective-permute-start(f32[750,16]{0,1:T(8,128)} %param.5), channel_id=1, source_target_pairs={{0,4},{4,8},{8,12},{12,16},{16,20},{20,24},{24,28},{28,0},{1,5},{5... | collective-permute-start | bytes 144008 | tf_op jit(solution)/shard_map/ppermute | solution.py:16
  3.6 5.3 %collective-permute-done = f32[750,16]{0,1:T(8,128)S(1)} collective-permute-done((f32[750,16]{0,1:T(8,128)}, f32[750,16]{0,1:T(8,128)S(1)}, u32[]{:S(2)}, u32[]{:S(2)}) %collective-permute-start) | collective-permute-done | bytes 48032 | tf_op jit(solution)/shard_map/ppermute | solution.py:16
  9.0 0.0 collective-permute-start.1
  9.0 6.8 %collective-permute-done.1 = f32[750,16]{0,1:T(8,128)S(1)} collective-permute-done((f32[750,16]{0,1:T(8,128)S(1)}, f32[750,16]{0,1:T(8,128)S(1)}, u32[]{:S(2)}, u32[]{:S(2)}) %collective-permute-start.1) | collective-permute-done | bytes 48032 | tf_op jit(solution)/shard_map/ppermute | solution.py:16
  15.8 0.0 collective-permute-start.2
  15.8 6.8 %collective-permute-done.2 = f32[750,16]{0,1:T(8,128)S(1)} collective-permute-done((f32[750,16]{0,1:T(8,128)S(1)}, f32[750,16]{0,1:T(8,128)S(1)}, u32[]{:S(2)}, u32[]{:S(2)}) %collective-permute-start.2) | collective-permute-done | bytes 48032 | tf_op jit(solution)/shard_map/ppermute | solution.py:16
  22.5 0.0 collective-permute-start.3
  22.5 6.8 %collective-permute-done.3 = f32[750,16]{0,1:T(8,128)S(1)} collective-permute-done((f32[750,16]{0,1:T(8,128)S(1)}, f32[750,16]{0,1:T(8,128)S(1)}, u32[]{:S(2)}, u32[]{:S(2)}) %collective-permute-start.3) | collective-permute-done | bytes 48032 | tf_op jit(solution)/shard_map/ppermute | solution.py:16
  29.3 0.0 collective-permute-start.4
  29.3 7.1 %collective-permute-done.4 = f32[750,16]{0,1:T(8,128)S(1)} collective-permute-done((f32[750,16]{0,1:T(8,128)S(1)}, f32[750,16]{0,1:T(8,128)S(1)}, u32[]{:S(2)}, u32[]{:S(2)}) %collective-permute-start.4) | collective-permute-done | bytes 48032 | tf_op jit(solution)/shard_map/ppermute | solution.py:16
  36.5 0.0 collective-permute-start.5
  36.5 1.2 fusion.5
  37.6 0.0 copy-start.1
  37.6 5.6 %collective-permute-done.5 = f32[750,16]{0,1:T(8,128)S(1)} collective-permute-done((f32[750,16]{0,1:T(8,128)S(1)}, f32[750,16]{0,1:T(8,128)S(1)}, u32[]{:S(2)}, u32[]{:S(2)}) %collective-permute-start.5) | collective-permute-done | bytes 48032 | tf_op jit(solution)/shard_map/ppermute | solution.py:16
  43.2 0.0 collective-permute-start.6
  43.2 1.2 fusion.7
  44.5 5.6 %collective-permute-done.6 = f32[750,16]{0,1:T(8,128)S(1)} collective-permute-done((f32[750,16]{0,1:T(8,128)S(1)}, f32[750,16]{0,1:T(8,128)S(1)}, u32[]{:S(2)}, u32[]{:S(2)}) %collective-permute-start.6) | collective-permute-done | bytes 48032 | tf_op jit(solution)/shard_map/ppermute | solution.py:16
  50.1 0.8 constant_dynamic-update-slice_fusion.8
  51.0 0.8 constant_dynamic-update-slice_fusion
  51.9 1.7 %fusion.3 = (f32[750]{0:T(1024)S(1)}, f32[1024,750]{0,1:T(8,128)S(1)}) fusion(f32[750,256]{0,1:T(8,128)S(1)} %constant_dynamic-update-slice_fusion, s32[]{:T(128)S(6)} %select_n.14, f32[750]{0:T(1024)S(1)} %rsqrt.25, bf16[1024,128]{1,0:T(8,128)(2,1)} %param.3, f32[1024]{0:T(1024)S(1)} %rsqrt.24), kind=kOutput, calls=%fused_computation.22 | convolution fusion | flops 198728464 | bytes 3738556 | tf_op jit(solution)/shard_map/dot_general | solution.py:63
  53.6 0.0 copy-done.1
  53.6 2.6 %multiply_reduce_fusion.11 = (f32[1024]{0:T(1024)S(1)}, f32[750]{0:T(1024)S(1)}, f32[1024,750]{0,1:T(8,128)}) fusion(f32[750,256]{0,1:T(8,128)S(1)} %constant_dynamic-update-slice_fusion, s32[]{:T(128)S(6)} %select_n.14, f32[750]{0:T(1024)S(1)} %rsqrt.25, bf16[1024,128]{1,0:T(8,128)(2,1)S(1)} %copy-done.1, f32[1024]{0:T(1024)S(1)} %rsqrt.26), kind=kOutput, calls=%fused_computation.20 | convolution fusion | flops 200263440 | bytes 3742652 | tf_op jit(solution)/shard_map/dot_general | solution.py:64
  56.2 17.4 %all-reduce.2 = (f32[750]{0:T(1024)S(1)}, f32[750]{0:T(1024)S(1)}) all-reduce(f32[750]{0:T(1024)S(1)} %get-tuple-element.30, f32[750]{0:T(1024)S(1)} %get-tuple-element.7), channel_id=1, replica_groups=mesh['ba'=8,'ka'=4] {'ba'}, use_global_device_ids=true, to_apply=%region_3.4 | all-reduce | flops 1500 | bytes 12000 | tf_op jit(solution)/shard_map/psum | solution.py:73
  73.6 0.7 multiply_reduce_fusion.10
  74.3 5.8 %all-reduce.7 = (f32[1024]{0:T(1024)S(1)}, f32[1024]{0:T(1024)S(1)}) all-reduce(f32[1024]{0:T(1024)S(1)} %get-tuple-element.6, f32[1024]{0:T(1024)S(1)} %get-tuple-element.9), channel_id=1, replica_groups=mesh['ba'=8,'ka'=4] {'ka'}, use_global_device_ids=true, to_apply=%region_16.17 | all-reduce | flops 2048 | bytes 16384 | tf_op jit(solution)/shard_map/pmax | solution.py:85
  80.1 2.9 %exponential_reduce_fusion.1 = (f32[1024]{0:T(1024)S(1)}, f32[1024]{0:T(1024)S(1)}) fusion(f32[1024,750]{0,1:T(8,128)} %get-tuple-element.32, f32[1024]{0:T(1024)S(1)} %get-tuple-element.27, f32[750]{0:T(1024)S(1)} %broadcast_divide_fusion.6), kind=kLoop, calls=%fused_computation.9 | loop fusion | flops 4605952 | bytes 3087288 | tf_op jit(solution)/shard_map/reduce_sum | solution.py:89
  83.0 7.1 %all-reduce.6 = (f32[1024]{0:T(1024)S(1)}, f32[1024]{0:T(1024)S(1)}) all-reduce(f32[1024]{0:T(1024)S(1)} %get-tuple-element.10, f32[1024]{0:T(1024)S(1)} %get-tuple-element.5), channel_id=1, replica_groups=mesh['ba'=8,'ka'=4] {'ka'}, use_global_device_ids=true, to_apply=%region_5.6 | all-reduce | flops 2048 | bytes 16384 | tf_op jit(solution)/shard_map/psum | solution.py:77
  90.1 2.4 %multiply_reduce_fusion.3 = f32[750]{0:T(1024)S(1)} fusion(f32[1024]{0:T(1024)S(1)} %get-tuple-element.33, f32[1024,750]{0,1:T(8,128)} %get-tuple-element.32), kind=kLoop, calls=%fused_computation.4 | loop fusion | flops 2303250 | bytes 3079096 | tf_op jit(solution)/shard_map/reduce_sum | solution.py:32
  92.5 0.6 multiply_reduce_fusion.8
  93.1 19.4 %all-reduce.1 = (f32[750]{0:T(1024)S(1)}, f32[750]{0:T(1024)S(1)}) all-reduce(f32[750]{0:T(1024)S(1)} %multiply_reduce_fusion.8, f32[750]{0:T(1024)S(1)} %multiply_reduce_fusion.3), channel_id=1, replica_groups=mesh['ba'=8,'ka'=4] {'ba'}, use_global_device_ids=true, to_apply=%region_7.8 | all-reduce | flops 1500 | bytes 12000 | tf_op jit(solution)/shard_map/psum | solution.py:73
  112.5 0.0 copy-start
  112.5 0.5 multiply_reduce_fusion.7
  113.1 1.3 copy-done
  114.4 0.5 multiply_reduce_fusion.2
  114.9 5.8 %all-reduce.5 = (f32[1024]{0:T(1024)S(1)}, f32[1024]{0:T(1024)S(1)}) all-reduce(f32[1024]{0:T(1024)S(1)} %multiply_reduce_fusion.7, f32[1024]{0:T(1024)S(1)} %multiply_reduce_fusion.2), channel_id=1, replica_groups=mesh['ba'=8,'ka'=4] {'ka'}, use_global_device_ids=true, to_apply=%region_9.10 | all-reduce | flops 2048 | bytes 16384 | tf_op jit(solution)/shard_map/psum | solution.py:77
  120.7 2.4 %multiply_reduce_fusion.1 = f32[750]{0:T(1024)S(1)} fusion(f32[1024]{0:T(1024)S(1)} %broadcast_divide_fusion, f32[1024,750]{0,1:T(8,128)} %get-tuple-element.32), kind=kLoop, calls=%fused_computation.2 | loop fusion | flops 2303250 | bytes 3079096 | tf_op jit(solution)/shard_map/reduce_sum | solution.py:32
  123.2 0.6 multiply_reduce_fusion.6
  123.7 17.4 %all-reduce = (f32[750]{0:T(1024)S(1)}, f32[750]{0:T(1024)S(1)}) all-reduce(f32[750]{0:T(1024)S(1)} %multiply_reduce_fusion.6, f32[750]{0:T(1024)S(1)} %multiply_reduce_fusion.1), channel_id=1, replica_groups=mesh['ba'=8,'ka'=4] {'ba'}, use_global_device_ids=true, to_apply=%region_11.12 | all-reduce | flops 1500 | bytes 12000 | tf_op jit(solution)/shard_map/psum | solution.py:73
  141.2 2.5 %fusion.2 = f32[1024]{0:T(1024)S(1)} fusion(f32[750]{0:T(1024)S(1)} %broadcast_divide_fusion.4, f32[1024]{0:T(1024)S(1)} %broadcast_divide_fusion, f32[1024,750]{0,1:T(8,128)} %get-tuple-element.32), kind=kLoop, calls=%fused_computation.18 | loop fusion | flops 3070976 | bytes 3083192 | tf_op jit(solution)/shard_map/reduce_sum | solution.py:82
  143.7 0.6 fusion.1
  144.3 5.8 %all-reduce.4 = (f32[1024]{0:T(1024)S(1)}, f32[1024]{0:T(1024)S(1)}) all-reduce(f32[1024]{0:T(1024)S(1)} %fusion.1, f32[1024]{0:T(1024)S(1)} %fusion.2), channel_id=1, replica_groups=mesh['ba'=8,'ka'=4] {'ka'}, use_global_device_ids=true, to_apply=%region_13.14 | all-reduce | flops 2048 | bytes 16384 | tf_op jit(solution)/shard_map/psum | solution.py:82
  150.1 5.4 %multiply_reduce_fusion.5 = (f32[1024]{0:T(1024)S(1)}, f32[1024]{0:T(1024)S(1)}, f32[1024]{0:T(1024)S(1)}, f32[1024,750]{0,1:T(8,128)}) fusion(f32[1024,750]{0,1:T(8,128)} %get-tuple-element.32, f32[1024]{0:T(1024)S(1)} %get-tuple-element.21, f32[1024]{0:T(1024)S(1)} %broadcast_divide_fusion.2, f32[750]{0:T(1024)S(1)} %broadcast_divide_fusion.7, ...), kind=kLoop, calls=%fused_computation.8 | loop fusion | flops 13052928 | bytes 9254768 | tf_op jit(solution)/shard_map/reduce_sum | solution.py:90
  155.5 10.5 %all-reduce.3 = (f32[1024]{0:T(1024)S(1)}, f32[1024]{0:T(1024)S(1)}, f32[1024]{0:T(1024)S(1)}, f32[1024]{0:T(1024)S(1)}) all-reduce(f32[1024]{0:T(1024)S(1)} %get-tuple-element.3, f32[1024]{0:T(1024)S(1)} %get-tuple-element.8, f32[1024]{0:T(1024)S(1)} %get-tuple-element.2, ...), channel_id=1, replica_groups=mesh['ba'=8,'ka'=4] {'ka'}, use_global_device_ids=true, to_apply=%region_38.39 | all-reduce | flops 4096 | bytes 32768 | tf_op jit(solution)/shard_map/psum | solution.py:86
  166.0 0.6 add_subtract_fusion
  (27 shorter events, 0.2 us)
Async XLA Ops:
  0.6 8.3 %collective-permute-start = (f32[750,16]{0,1:T(8,128)}, f32[750,16]{0,1:T(8,128)S(1)}, u32[]{:S(2)}, u32[]{:S(2)}) collective-permute-start(f32[750,16]{0,1:T(8,128)} %param.5), channel_id=1, source_target_pairs={{0,4},{4,8},{8,12},{12,16},{16,20},{20,24},{24,28},{28,0},{1,5},{5... | collective-permute-start | bytes 144008 | tf_op jit(solution)/shard_map/ppermute | solution.py:16
  9.0 6.8 %collective-permute-start.1 = (f32[750,16]{0,1:T(8,128)S(1)}, f32[750,16]{0,1:T(8,128)S(1)}, u32[]{:S(2)}, u32[]{:S(2)}) collective-permute-start(f32[750,16]{0,1:T(8,128)S(1)} %collective-permute-done), channel_id=1, source_target_pairs={{0,4},{4,8},{8,12},{12,16},{16,20},{20,24},{24,28},{28,0},{1,5},{5... | collective-permute-start | bytes 144008 | tf_op jit(solution)/shard_map/ppermute | solution.py:16
  15.8 6.8 %collective-permute-start.2 = (f32[750,16]{0,1:T(8,128)S(1)}, f32[750,16]{0,1:T(8,128)S(1)}, u32[]{:S(2)}, u32[]{:S(2)}) collective-permute-start(f32[750,16]{0,1:T(8,128)S(1)} %collective-permute-done.1), channel_id=1, source_target_pairs={{0,4},{4,8},{8,12},{12,16},{16,20},{20,24},{24,28},{28,0},{1,5},{5... | collective-permute-start | bytes 144008 | tf_op jit(solution)/shard_map/ppermute | solution.py:16
  22.5 6.8 %collective-permute-start.3 = (f32[750,16]{0,1:T(8,128)S(1)}, f32[750,16]{0,1:T(8,128)S(1)}, u32[]{:S(2)}, u32[]{:S(2)}) collective-permute-start(f32[750,16]{0,1:T(8,128)S(1)} %collective-permute-done.2), channel_id=1, source_target_pairs={{0,4},{4,8},{8,12},{12,16},{16,20},{20,24},{24,28},{28,0},{1,5},{5... | collective-permute-start | bytes 144008 | tf_op jit(solution)/shard_map/ppermute | solution.py:16
  29.3 7.1 %collective-permute-start.4 = (f32[750,16]{0,1:T(8,128)S(1)}, f32[750,16]{0,1:T(8,128)S(1)}, u32[]{:S(2)}, u32[]{:S(2)}) collective-permute-start(f32[750,16]{0,1:T(8,128)S(1)} %collective-permute-done.3), channel_id=1, source_target_pairs={{0,4},{4,8},{8,12},{12,16},{16,20},{20,24},{24,28},{28,0},{1,5},{5... | collective-permute-start | bytes 144008 | tf_op jit(solution)/shard_map/ppermute | solution.py:16
  36.5 6.8 %collective-permute-start.5 = (f32[750,16]{0,1:T(8,128)S(1)}, f32[750,16]{0,1:T(8,128)S(1)}, u32[]{:S(2)}, u32[]{:S(2)}) collective-permute-start(f32[750,16]{0,1:T(8,128)S(1)} %collective-permute-done.4), channel_id=1, source_target_pairs={{0,4},{4,8},{8,12},{12,16},{16,20},{20,24},{24,28},{28,0},{1,5},{5... | collective-permute-start | bytes 144008 | tf_op jit(solution)/shard_map/ppermute | solution.py:16
  37.6 16.0 %copy-start.1 = (bf16[1024,128]{1,0:T(8,128)(2,1)S(1)}, bf16[1024,128]{1,0:T(8,128)(2,1)}, u32[]{:S(2)}) copy-start(bf16[1024,128]{1,0:T(8,128)(2,1)} %param.4) | copy-start | bytes 786436
  43.2 6.8 %collective-permute-start.6 = (f32[750,16]{0,1:T(8,128)S(1)}, f32[750,16]{0,1:T(8,128)S(1)}, u32[]{:S(2)}, u32[]{:S(2)}) collective-permute-start(f32[750,16]{0,1:T(8,128)S(1)} %collective-permute-done.5), channel_id=1, source_target_pairs={{0,4},{4,8},{8,12},{12,16},{16,20},{20,24},{24,28},{28,0},{1,5},{5... | collective-permute-start | bytes 144008 | tf_op jit(solution)/shard_map/ppermute | solution.py:16
  112.5 1.9 %copy-start = (f32[1024,750]{0,1:T(8,128)S(1)}, f32[1024,750]{0,1:T(8,128)}, u32[]{:S(2)}) copy-start(f32[1024,750]{0,1:T(8,128)} %get-tuple-element.32) | copy-start | bytes 9216004
